TPU v7x, 32 devices: a whole 2x2x4 slice. The times are simulated.
32 devices in a mesh: row: 8 (over y, x, core), col: 4 (over z).
Axes of the slice: x: 2, y: 2, z: 4, core: 2. Of those that a mesh axis runs over, the one named last changes fastest.
Arguments:
- inputs: int32 [8, 128, 128], replicated, may hold values 0 or 1
- targets: int32 [8, 128, 128], replicated, may hold values 0 or 1
- initial_spikes: int32 [128, 128, 128], P(None, 'row'), may hold values 0 or 1
- w_in: bfloat16 [128, 128, 128], P(None, 'row'), may hold values from -0.5 to 0.5
- w_rec: bfloat16 [128, 128, 128, 128], P(None, 'col', 'row'), may hold values from -0.046875 to 0.046875
- w_out: bfloat16 [128, 128, 128], P('row'), may hold values from -0.046875 to 0.046875
- feedback: bfloat16 [128, 128, 128], P(None, 'row')
- adapt_gain: float32 [128, 128], P('row'), may hold values from 0.1 to 2
- adapt_decay: float32 [128, 128], P('row'), may hold values from 0.8 to 0.99
Outputs:
- readout: float32 [8, 128, 128], replicated
- grad_clipped: float32 [128, 128, 128, 128], P(None, 'col', 'row')
All inputs are finite; a program needn't handle non-finite values. No bound on the sum of `initial_spikes` on one device may be relied on, other than what follows from the above.
Results may differ from a plain program's by a relative error of at most 0.0015.
Values may be sent and summed in bfloat16 or wider, within the bound.
No kernel may reach another device: no remote copies, remote signals or barrier semaphores. Data moves between devices by JAX's collectives and lax.ppermute only.
A program may use at most 128 MiB of HBM per device.

v0:
```python
import jax
import jax.numpy as jnp
from jax import lax
from jax.sharding import PartitionSpec as P

NA = 128
NB = 128
cellular_leak_multiplier = 0.8
readout_decay = 0.8


def body(inputs, targets, initial_spikes, w_in, w_rec, w_out, feedback, adapt_gain, adapt_decay):
    steps_count, batch, channels = inputs.shape
    own_cols = w_rec.shape[1]
    rows_loc = w_rec.shape[2]
    entire_column_set = w_rec.shape[3]
    col_start = lax.axis_index("col") * own_cols
    rows_all = steps_count * batch

    def own_part(array, axis_dim):
        return lax.dynamic_slice_in_dim(array, col_start, own_cols, axis_dim)

    def select_cols(array, axis_dim):
        return own_part(array, axis_dim)

    def combine_currents(partial_value):
        return lax.psum_scatter(partial_value, "col", scatter_dimension=2, tiled=True)

    weights = w_rec.reshape(w_rec.shape[0] * own_cols, rows_loc * entire_column_set)
    w_in_loc = select_cols(w_in, 2)
    state_cols = w_in_loc.shape[2]
    external = jnp.dot(
        inputs.reshape(rows_all, channels).astype(jnp.bfloat16),
        w_in_loc.reshape(channels, -1),
        preferred_element_type=jnp.float32,
    ).reshape(steps_count, batch, rows_loc, state_cols)
    coupling_magnitude = select_cols(adapt_gain, 1)
    retention = select_cols(adapt_decay, 1)
    start_spikes = select_cols(initial_spikes, 2).astype(jnp.bfloat16)

    def advance(state, drive_now):
        pulse_output, cellular_charge, barrier_shift_amount, sender_trace = state
        arrivals = lax.all_gather(pulse_output, "row", axis=1, tiled=True).reshape(batch, -1)
        sender_trace = cellular_leak_multiplier * sender_trace + arrivals.astype(jnp.float32)
        partial_value = jnp.dot(arrivals, weights, preferred_element_type=jnp.float32).reshape(
            batch, rows_loc, entire_column_set
        )
        current = drive_now + combine_currents(partial_value)
        spike_float = pulse_output.astype(jnp.float32)
        cellular_charge = cellular_leak_multiplier * cellular_charge + current - spike_float
        barrier_shift_amount = retention * barrier_shift_amount + spike_float
        present_emission_frequency = jax.nn.sigmoid(
            cellular_charge - 1.0 - coupling_magnitude * barrier_shift_amount
        )
        surrogate_slope = present_emission_frequency * (1.0 - present_emission_frequency)
        pulse_output = present_emission_frequency.astype(jnp.bfloat16)
        return (
            (pulse_output, cellular_charge, barrier_shift_amount, sender_trace),
            (sender_trace.astype(jnp.bfloat16), surrogate_slope, pulse_output),
        )

    zeros = jnp.zeros((batch, rows_loc, state_cols), jnp.float32)
    trace_zero = jnp.zeros((batch, weights.shape[0]), jnp.float32)
    _, (traces, slopes, spikes) = lax.scan(
        advance, (start_spikes, zeros, zeros, trace_zero), external
    )
    readout_loc = own_part(w_out, 1).reshape(rows_loc * own_cols, -1)
    projected = lax.psum(
        jnp.dot(spikes.reshape(rows_all, -1), readout_loc, preferred_element_type=jnp.float32),
        ("row", "col"),
    )
    outputs_n = readout_loc.shape[1]
    projected = projected.reshape(steps_count, batch, outputs_n)

    def smooth(level, incoming):
        level = readout_decay * level + incoming
        return (level, level)

    _, readout = lax.scan(smooth, jnp.zeros((batch, outputs_n), jnp.float32), projected)
    errors = (jax.nn.sigmoid(readout) - targets.astype(jnp.float32)).reshape(rows_all, outputs_n)
    err_high = errors.astype(jnp.bfloat16)
    err_low = (errors - err_high.astype(jnp.float32)).astype(jnp.bfloat16)
    feedback_loc = select_cols(feedback, 2).reshape(outputs_n, -1)
    signal = jnp.dot(err_high, feedback_loc, preferred_element_type=jnp.float32) + jnp.dot(
        err_low, feedback_loc, preferred_element_type=jnp.float32
    )
    signal = signal.reshape(steps_count, batch, rows_loc, state_cols)
    weighted = signal * slopes
    decays = retention - slopes * coupling_magnitude

    def backward(carried, inputs_now):
        weighted_now, decay_now = inputs_now
        return (weighted_now + decay_now * carried, carried)

    _, future = lax.scan(backward, zeros, (weighted, decays), reverse=True)
    factors = (weighted - coupling_magnitude * slopes * future).astype(jnp.bfloat16)
    traces_flat = traces.reshape(rows_all, -1)
    pieces = lax.all_gather(
        factors.reshape(rows_all, rows_loc, state_cols), "col", axis=2, tiled=True
    )
    product = lax.dot_general(
        traces_flat,
        pieces.reshape(rows_all, -1),
        (((0,), (0,)), ((), ())),
        preferred_element_type=jnp.float32,
    )
    grad = product.reshape(-1, rows_loc, pieces.shape[2])
    squares = lax.psum(jnp.sum(grad * grad), ("row", "col"))
    clip_factor = jnp.minimum(1.0, NA * NB / 16.0 / jnp.sqrt(squares + 1e-06))
    return (readout, (grad * clip_factor).reshape(w_rec.shape))


def solution(mesh):
    return jax.shard_map(
        body,
        mesh=mesh,
        in_specs=(
            P(),
            P(),
            P(None, "row", None),
            P(None, "row", None),
            P(None, "col", "row", None),
            P("row", None, None),
            P(None, "row", None),
            P("row", None),
            P("row", None),
        ),
        out_specs=(P(), P(None, "col", "row", None)),
        check_vma=False,
    )
```

profile of v0, /device:TPU:0, one launch (start us, length us, event | category | flops | bytes accessed | tf_op | source)
XLA Modules:
  0.0 1113.9 jit_solution(2757752575109716151)
XLA Ops:
  15.9 17.2 %copy.96 = bf16[512,8,16,128]{3,1,2,0:T(8,128)(2,1)} copy(bf16[512,8,16,128]{3,2,1,0:T(8,128)(2,1)} %bitcast.115) | data formatting | bytes 33554432
  33.1 21.2 %copy.58 = bf16[4096,2048]{0,1:T(8,128)(2,1)} copy(bf16[4096,2048]{1,0:T(8,128)(2,1)} %bitcast.112) | data formatting | bytes 33554432
  55.9 592.0 %while.55 = (s32[]{:T(128)}, bf16[128,16,32]{0,2,1:T(8,128)(2,1)S(1)}, f32[128,16,32]{0,2,1:T(8,128)S(1)}, f32[128,16,32]{0,2,1:T(8,128)S(1)}, f32[128,4096]{0,1...) while((s32[]{:T(128)}, ...), condition=%wide.region_2.3_spmd.clone, body=%wide.region_0.2_spmd.clone.sunk | while | flops 2151677952 | bytes 45881672 | solution.py:64
  56.7 28.0 %all-gather.5.cloned.1.call-done = bf16[128,128,32]{0,2,1:T(8,128)(2,1)} async-done(((bf16[128,16,32]{0,2,1:T(8,128)(2,1)}), bf16[128,128,32]{0,2,1:T(8,128)(2,1)}) %all-gather.5.cloned.1.call-update) | async-done | bytes 1048592 | tf_op jit(solution)/shard_map/while/body/eval_jaxpr/all_gather | solution.py:43
  84.7 11.6 %fusion.29 = f32[128,16,128]{0,2,1:T(8,128)} fusion(bf16[128,4096,1]{0,1,2:T(8,128)(2,1)} %bitcast.111, bf16[16,128,4096]{2,1,0:T(8,128)(2,1)} %bitcast.109), kind=kOutput, calls=%fused_computation.43.clone.1 | convolution fusion | flops 2147483648 | bytes 18874368 | tf_op jit(solution)/shard_map/while/body/eval_jaxpr/dot_general | solution.py:45
  101.7 22.1 %reduce-scatter.2.cloned.1.call-done = f32[128,16,32]{0,2,1:T(8,128)} async-done(((f32[128,16,128]{0,2,1:T(8,128)}), f32[128,16,32]{0,2,1:T(8,128)}) %reduce-scatter.2.cloned.1.call-update) | async-done | bytes 262160 | tf_op jit(solution)/shard_map/while/body/eval_jaxpr/reduce_scatter | solution.py:27
  126.0 7.7 dynamic_update_slice.49
  134.5 23.8 %all-gather.5.cloned.1.call-done = bf16[128,128,32]{0,2,1:T(8,128)(2,1)} async-done(((bf16[128,16,32]{0,2,1:T(8,128)(2,1)}), bf16[128,128,32]{0,2,1:T(8,128)(2,1)}) %all-gather.5.cloned.1.call-update) | async-done | bytes 1048592 | tf_op jit(solution)/shard_map/while/body/eval_jaxpr/all_gather | solution.py:43
  158.3 11.6 %fusion.29 = f32[128,16,128]{0,2,1:T(8,128)} fusion(bf16[128,4096,1]{0,1,2:T(8,128)(2,1)} %bitcast.111, bf16[16,128,4096]{2,1,0:T(8,128)(2,1)} %bitcast.109), kind=kOutput, calls=%fused_computation.43.clone.1 | convolution fusion | flops 2147483648 | bytes 18874368 | tf_op jit(solution)/shard_map/while/body/eval_jaxpr/dot_general | solution.py:45
  176.8 20.5 %reduce-scatter.2.cloned.1.call-done = f32[128,16,32]{0,2,1:T(8,128)} async-done(((f32[128,16,128]{0,2,1:T(8,128)}), f32[128,16,32]{0,2,1:T(8,128)}) %reduce-scatter.2.cloned.1.call-update) | async-done | bytes 262160 | tf_op jit(solution)/shard_map/while/body/eval_jaxpr/reduce_scatter | solution.py:27
  199.5 7.7 dynamic_update_slice.49
  207.9 23.6 %all-gather.5.cloned.1.call-done = bf16[128,128,32]{0,2,1:T(8,128)(2,1)} async-done(((bf16[128,16,32]{0,2,1:T(8,128)(2,1)}), bf16[128,128,32]{0,2,1:T(8,128)(2,1)}) %all-gather.5.cloned.1.call-update) | async-done | bytes 1048592 | tf_op jit(solution)/shard_map/while/body/eval_jaxpr/all_gather | solution.py:43
  231.5 11.6 %fusion.29 = f32[128,16,128]{0,2,1:T(8,128)} fusion(bf16[128,4096,1]{0,1,2:T(8,128)(2,1)} %bitcast.111, bf16[16,128,4096]{2,1,0:T(8,128)(2,1)} %bitcast.109), kind=kOutput, calls=%fused_computation.43.clone.1 | convolution fusion | flops 2147483648 | bytes 18874368 | tf_op jit(solution)/shard_map/while/body/eval_jaxpr/dot_general | solution.py:45
  250.1 20.5 %reduce-scatter.2.cloned.1.call-done = f32[128,16,32]{0,2,1:T(8,128)} async-done(((f32[128,16,128]{0,2,1:T(8,128)}), f32[128,16,32]{0,2,1:T(8,128)}) %reduce-scatter.2.cloned.1.call-update) | async-done | bytes 262160 | tf_op jit(solution)/shard_map/while/body/eval_jaxpr/reduce_scatter | solution.py:27
  272.7 7.7 dynamic_update_slice.49
  281.2 23.8 %all-gather.5.cloned.1.call-done = bf16[128,128,32]{0,2,1:T(8,128)(2,1)} async-done(((bf16[128,16,32]{0,2,1:T(8,128)(2,1)}), bf16[128,128,32]{0,2,1:T(8,128)(2,1)}) %all-gather.5.cloned.1.call-update) | async-done | bytes 1048592 | tf_op jit(solution)/shard_map/while/body/eval_jaxpr/all_gather | solution.py:43
  305.1 11.6 %fusion.29 = f32[128,16,128]{0,2,1:T(8,128)} fusion(bf16[128,4096,1]{0,1,2:T(8,128)(2,1)} %bitcast.111, bf16[16,128,4096]{2,1,0:T(8,128)(2,1)} %bitcast.109), kind=kOutput, calls=%fused_computation.43.clone.1 | convolution fusion | flops 2147483648 | bytes 18874368 | tf_op jit(solution)/shard_map/while/body/eval_jaxpr/dot_general | solution.py:45
  323.6 20.5 %reduce-scatter.2.cloned.1.call-done = f32[128,16,32]{0,2,1:T(8,128)} async-done(((f32[128,16,128]{0,2,1:T(8,128)}), f32[128,16,32]{0,2,1:T(8,128)}) %reduce-scatter.2.cloned.1.call-update) | async-done | bytes 262160 | tf_op jit(solution)/shard_map/while/body/eval_jaxpr/reduce_scatter | solution.py:27
  346.3 7.7 dynamic_update_slice.49
  354.8 23.8 %all-gather.5.cloned.1.call-done = bf16[128,128,32]{0,2,1:T(8,128)(2,1)} async-done(((bf16[128,16,32]{0,2,1:T(8,128)(2,1)}), bf16[128,128,32]{0,2,1:T(8,128)(2,1)}) %all-gather.5.cloned.1.call-update) | async-done | bytes 1048592 | tf_op jit(solution)/shard_map/while/body/eval_jaxpr/all_gather | solution.py:43
  378.6 11.6 %fusion.29 = f32[128,16,128]{0,2,1:T(8,128)} fusion(bf16[128,4096,1]{0,1,2:T(8,128)(2,1)} %bitcast.111, bf16[16,128,4096]{2,1,0:T(8,128)(2,1)} %bitcast.109), kind=kOutput, calls=%fused_computation.43.clone.1 | convolution fusion | flops 2147483648 | bytes 18874368 | tf_op jit(solution)/shard_map/while/body/eval_jaxpr/dot_general | solution.py:45
  397.2 20.5 %reduce-scatter.2.cloned.1.call-done = f32[128,16,32]{0,2,1:T(8,128)} async-done(((f32[128,16,128]{0,2,1:T(8,128)}), f32[128,16,32]{0,2,1:T(8,128)}) %reduce-scatter.2.cloned.1.call-update) | async-done | bytes 262160 | tf_op jit(solution)/shard_map/while/body/eval_jaxpr/reduce_scatter | solution.py:27
  419.9 7.7 dynamic_update_slice.49
  428.3 23.8 %all-gather.5.cloned.1.call-done = bf16[128,128,32]{0,2,1:T(8,128)(2,1)} async-done(((bf16[128,16,32]{0,2,1:T(8,128)(2,1)}), bf16[128,128,32]{0,2,1:T(8,128)(2,1)}) %all-gather.5.cloned.1.call-update) | async-done | bytes 1048592 | tf_op jit(solution)/shard_map/while/body/eval_jaxpr/all_gather | solution.py:43
  452.2 11.6 %fusion.29 = f32[128,16,128]{0,2,1:T(8,128)} fusion(bf16[128,4096,1]{0,1,2:T(8,128)(2,1)} %bitcast.111, bf16[16,128,4096]{2,1,0:T(8,128)(2,1)} %bitcast.109), kind=kOutput, calls=%fused_computation.43.clone.1 | convolution fusion | flops 2147483648 | bytes 18874368 | tf_op jit(solution)/shard_map/while/body/eval_jaxpr/dot_general | solution.py:45
  470.7 20.5 %reduce-scatter.2.cloned.1.call-done = f32[128,16,32]{0,2,1:T(8,128)} async-done(((f32[128,16,128]{0,2,1:T(8,128)}), f32[128,16,32]{0,2,1:T(8,128)}) %reduce-scatter.2.cloned.1.call-update) | async-done | bytes 262160 | tf_op jit(solution)/shard_map/while/body/eval_jaxpr/reduce_scatter | solution.py:27
  493.4 7.7 dynamic_update_slice.49
  501.9 23.8 %all-gather.5.cloned.1.call-done = bf16[128,128,32]{0,2,1:T(8,128)(2,1)} async-done(((bf16[128,16,32]{0,2,1:T(8,128)(2,1)}), bf16[128,128,32]{0,2,1:T(8,128)(2,1)}) %all-gather.5.cloned.1.call-update) | async-done | bytes 1048592 | tf_op jit(solution)/shard_map/while/body/eval_jaxpr/all_gather | solution.py:43
  525.7 11.6 %fusion.29 = f32[128,16,128]{0,2,1:T(8,128)} fusion(bf16[128,4096,1]{0,1,2:T(8,128)(2,1)} %bitcast.111, bf16[16,128,4096]{2,1,0:T(8,128)(2,1)} %bitcast.109), kind=kOutput, calls=%fused_computation.43.clone.1 | convolution fusion | flops 2147483648 | bytes 18874368 | tf_op jit(solution)/shard_map/while/body/eval_jaxpr/dot_general | solution.py:45
  544.2 20.6 %reduce-scatter.2.cloned.1.call-done = f32[128,16,32]{0,2,1:T(8,128)} async-done(((f32[128,16,128]{0,2,1:T(8,128)}), f32[128,16,32]{0,2,1:T(8,128)}) %reduce-scatter.2.cloned.1.call-update) | async-done | bytes 262160 | tf_op jit(solution)/shard_map/while/body/eval_jaxpr/reduce_scatter | solution.py:27
  566.9 7.7 dynamic_update_slice.49
  575.4 23.6 %all-gather.5.cloned.1.call-done = bf16[128,128,32]{0,2,1:T(8,128)(2,1)} async-done(((bf16[128,16,32]{0,2,1:T(8,128)(2,1)}), bf16[128,128,32]{0,2,1:T(8,128)(2,1)}) %all-gather.5.cloned.1.call-update) | async-done | bytes 1048592 | tf_op jit(solution)/shard_map/while/body/eval_jaxpr/all_gather | solution.py:43
  598.9 11.6 %fusion.29 = f32[128,16,128]{0,2,1:T(8,128)} fusion(bf16[128,4096,1]{0,1,2:T(8,128)(2,1)} %bitcast.111, bf16[16,128,4096]{2,1,0:T(8,128)(2,1)} %bitcast.109), kind=kOutput, calls=%fused_computation.43.clone.1 | convolution fusion | flops 2147483648 | bytes 18874368 | tf_op jit(solution)/shard_map/while/body/eval_jaxpr/dot_general | solution.py:45
  617.5 20.5 %reduce-scatter.2.cloned.1.call-done = f32[128,16,32]{0,2,1:T(8,128)} async-done(((f32[128,16,128]{0,2,1:T(8,128)}), f32[128,16,32]{0,2,1:T(8,128)}) %reduce-scatter.2.cloned.1.call-update) | async-done | bytes 262160 | tf_op jit(solution)/shard_map/while/body/eval_jaxpr/reduce_scatter | solution.py:27
  640.2 7.7 dynamic_update_slice.49
  651.9 129.3 %all-reduce.2.cloned.1.call-done = f32[8,128,128]{2,1,0:T(8,128)} async-done(((f32[8,128,128]{2,1,0:T(8,128)}), f32[8,128,128]{2,1,0:T(8,128)}) %all-reduce.2.cloned.1.call-update) | async-done | bytes 524304 | tf_op jit(solution)/shard_map/psum | solution.py:68
  798.2 112.8 %while.57 = (s32[]{:T(128)}, f32[128,16,32]{2,1,0:T(8,128)}, f32[8,128,16,32]{1,0,3,2:T(8,128)}, f32[8,128,16,32]{1,0,3,2:T(8,128)}, f32[8,128,16,32]{1,0,3,2:T(8,128)}, /*index=5*/s32[]{:T(128)}, s32[]{:T(128)}, s32[]{:T(128)}) while((s32[]{:T(128)}, f32[128,16,32]{2,1,0:T(8,128)}, f32[8,128,16,32]{1,0,3,2:T(8,128)}, ...), condition=%wide.region_7.8_spmd.clone, body=%wide.region_6.7_spmd.clone.sunk | while | flops 196612 | bytes 4456571 | solution.py:95
  803.5 7.7 dynamic_update_slice.51
  817.8 7.7 dynamic_update_slice.51
  832.0 7.7 dynamic_update_slice.51
  874.8 7.7 dynamic_update_slice.51
  889.0 7.7 dynamic_update_slice.51
  903.3 7.7 dynamic_update_slice.51
  915.5 79.8 %all-gather.3.cloned.1.call-done = bf16[1024,16,128]{0,2,1:T(8,128)(2,1)} async-done(((bf16[1024,16,32]{0,2,1:T(8,128)(2,1)}), bf16[1024,16,128]{0,2,1:T(8,128)(2,1)}) %all-gather.3.cloned.1.call-update) | async-done | bytes 4194320 | tf_op jit(solution)/shard_map/all_gather | solution.py:98
  995.3 26.1 %multiply_reduce_fusion = (f32[]{:T(128)}, f32[4096,16,128]{2,0,1:T(8,128)}) fusion(bf16[1024,4096,1]{1,0,2:T(8,128)(2,1)} %bitcast.128, bf16[1024,16,128]{0,2,1:T(8,128)(2,1)} %all-gather.3.cloned.1.call-done), kind=kOutput, calls=%fused_computation.22 | convolution fusion | flops 17196646400 | bytes 46137348 | tf_op jit(solution)/shard_map/dot_general | solution.py:101
  1021.4 39.1 %psum.15 = f32[]{:T(128)} all-reduce(f32[]{:T(128)} %get-tuple-element.484), channel_id=1, replica_groups=mesh['row'=8,'col'=4] {'row','col'}, use_global_device_ids=true, to_apply=%region_9.10 | all-reduce | flops 1 | bytes 8 | tf_op jit(solution)/shard_map/psum | solution.py:108
  1061.2 11.9 %broadcast_multiply_fusion = f32[4096,16,128]{2,0,1:T(8,128)S(1)} fusion(f32[4096,16,128]{2,0,1:T(8,128)} %get-tuple-element.485, f32[]{:T(128)S(6)} %min.3), kind=kLoop, calls=%fused_computation.24 | loop fusion | flops 8388608 | bytes 67108864 | tf_op jit(solution)/shard_map/mul | solution.py:110
  1073.1 33.7 %copy.69 = f32[128,32,16,128]{3,2,1,0:T(8,128)} copy(f32[128,32,16,128]{3,1,0,2:T(8,128)S(1)} %bitcast.110) | data formatting | bytes 67108864
  (230 shorter events, 185.1 us)
Async XLA Ops:
  8.0 2.8 copy-start
  33.1 21.2 %copy-start.9 = (f32[16,128]{1,0:T(8,128)S(1)}, f32[16,128]{1,0:T(8,128)}, u32[]{:S(2)}) copy-start(f32[16,128]{1,0:T(8,128)} %param.23) | copy-start | bytes 24580
  33.1 21.2 %copy-start.10 = (f32[16,128]{1,0:T(8,128)S(1)}, f32[16,128]{1,0:T(8,128)}, u32[]{:S(2)}) copy-start(f32[16,128]{1,0:T(8,128)} %param.22) | copy-start | bytes 24580
  55.9 28.8 %all-gather.5.cloned.1.call-start = ((), (), s32[]{:S(2)}) async-start(), calls=%async_computation.3 | async-start | bytes 1179648 | tf_op jit(solution)/shard_map/while/body/eval_jaxpr/all_gather | solution.py:43
  56.6 67.2 %reduce-scatter.2.cloned.1.call-start = ((), (), s32[]{:S(2)}) async-start(), calls=%async_computation.4 | async-start | bytes 1310720 | tf_op jit(solution)/shard_map/while/body/eval_jaxpr/reduce_scatter | solution.py:27
  96.3 1.9 copy-start.2
  100.1 23.7 %copy-start.5 = (bf16[128,16,32]{0,2,1:T(8,128)(2,1)S(1)}, bf16[128,16,32]{0,2,1:T(8,128)(2,1)}, u32[]{:S(2)}) copy-start(bf16[128,16,32]{0,2,1:T(8,128)(2,1)} %copy-done.4) | copy-start | bytes 393220 | tf_op jit(solution)/shard_map/while
  133.7 0.6 copy-start.4
  133.7 24.6 %all-gather.5.cloned.1.call-start = ((), (), s32[]{:S(2)}) async-start(), calls=%async_computation.3 | async-start | bytes 1179648 | tf_op jit(solution)/shard_map/while/body/eval_jaxpr/all_gather | solution.py:43
  134.4 62.9 %reduce-scatter.2.cloned.1.call-start = ((), (), s32[]{:S(2)}) async-start(), calls=%async_computation.4 | async-start | bytes 1310720 | tf_op jit(solution)/shard_map/while/body/eval_jaxpr/reduce_scatter | solution.py:27
  169.9 1.9 copy-start.2
  175.2 22.2 %copy-start.5 = (bf16[128,16,32]{0,2,1:T(8,128)(2,1)S(1)}, bf16[128,16,32]{0,2,1:T(8,128)(2,1)}, u32[]{:S(2)}) copy-start(bf16[128,16,32]{0,2,1:T(8,128)(2,1)} %copy-done.4) | copy-start | bytes 393220 | tf_op jit(solution)/shard_map/while
  207.2 0.6 copy-start.4
  207.2 24.3 %all-gather.5.cloned.1.call-start = ((), (), s32[]{:S(2)}) async-start(), calls=%async_computation.3 | async-start | bytes 1179648 | tf_op jit(solution)/shard_map/while/body/eval_jaxpr/all_gather | solution.py:43
  207.9 62.7 %reduce-scatter.2.cloned.1.call-start = ((), (), s32[]{:S(2)}) async-start(), calls=%async_computation.4 | async-start | bytes 1310720 | tf_op jit(solution)/shard_map/while/body/eval_jaxpr/reduce_scatter | solution.py:27
  243.1 1.9 copy-start.2
  248.4 22.2 %copy-start.5 = (bf16[128,16,32]{0,2,1:T(8,128)(2,1)S(1)}, bf16[128,16,32]{0,2,1:T(8,128)(2,1)}, u32[]{:S(2)}) copy-start(bf16[128,16,32]{0,2,1:T(8,128)(2,1)} %copy-done.4) | copy-start | bytes 393220 | tf_op jit(solution)/shard_map/while
  280.5 0.6 copy-start.4
  280.5 24.6 %all-gather.5.cloned.1.call-start = ((), (), s32[]{:S(2)}) async-start(), calls=%async_computation.3 | async-start | bytes 1179648 | tf_op jit(solution)/shard_map/while/body/eval_jaxpr/all_gather | solution.py:43
  281.2 62.9 %reduce-scatter.2.cloned.1.call-start = ((), (), s32[]{:S(2)}) async-start(), calls=%async_computation.4 | async-start | bytes 1310720 | tf_op jit(solution)/shard_map/while/body/eval_jaxpr/reduce_scatter | solution.py:27
  316.7 1.9 copy-start.2
  322.0 22.2 %copy-start.5 = (bf16[128,16,32]{0,2,1:T(8,128)(2,1)S(1)}, bf16[128,16,32]{0,2,1:T(8,128)(2,1)}, u32[]{:S(2)}) copy-start(bf16[128,16,32]{0,2,1:T(8,128)(2,1)} %copy-done.4) | copy-start | bytes 393220 | tf_op jit(solution)/shard_map/while
  354.0 0.6 copy-start.4
  354.0 24.6 %all-gather.5.cloned.1.call-start = ((), (), s32[]{:S(2)}) async-start(), calls=%async_computation.3 | async-start | bytes 1179648 | tf_op jit(solution)/shard_map/while/body/eval_jaxpr/all_gather | solution.py:43
  354.7 62.9 %reduce-scatter.2.cloned.1.call-start = ((), (), s32[]{:S(2)}) async-start(), calls=%async_computation.4 | async-start | bytes 1310720 | tf_op jit(solution)/shard_map/while/body/eval_jaxpr/reduce_scatter | solution.py:27
  390.2 1.9 copy-start.2
  395.5 22.2 %copy-start.5 = (bf16[128,16,32]{0,2,1:T(8,128)(2,1)S(1)}, bf16[128,16,32]{0,2,1:T(8,128)(2,1)}, u32[]{:S(2)}) copy-start(bf16[128,16,32]{0,2,1:T(8,128)(2,1)} %copy-done.4) | copy-start | bytes 393220 | tf_op jit(solution)/shard_map/while
  427.6 24.6 %all-gather.5.cloned.1.call-start = ((), (), s32[]{:S(2)}) async-start(), calls=%async_computation.3 | async-start | bytes 1179648 | tf_op jit(solution)/shard_map/while/body/eval_jaxpr/all_gather | solution.py:43
  428.3 62.9 %reduce-scatter.2.cloned.1.call-start = ((), (), s32[]{:S(2)}) async-start(), calls=%async_computation.4 | async-start | bytes 1310720 | tf_op jit(solution)/shard_map/while/body/eval_jaxpr/reduce_scatter | solution.py:27
  463.8 1.9 copy-start.2
  469.1 22.2 %copy-start.5 = (bf16[128,16,32]{0,2,1:T(8,128)(2,1)S(1)}, bf16[128,16,32]{0,2,1:T(8,128)(2,1)}, u32[]{:S(2)}) copy-start(bf16[128,16,32]{0,2,1:T(8,128)(2,1)} %copy-done.4) | copy-start | bytes 393220 | tf_op jit(solution)/shard_map/while
  501.1 0.6 copy-start.4
  501.1 24.6 %all-gather.5.cloned.1.call-start = ((), (), s32[]{:S(2)}) async-start(), calls=%async_computation.3 | async-start | bytes 1179648 | tf_op jit(solution)/shard_map/while/body/eval_jaxpr/all_gather | solution.py:43
  501.8 62.9 %reduce-scatter.2.cloned.1.call-start = ((), (), s32[]{:S(2)}) async-start(), calls=%async_computation.4 | async-start | bytes 1310720 | tf_op jit(solution)/shard_map/while/body/eval_jaxpr/reduce_scatter | solution.py:27
  537.3 1.9 copy-start.2
  542.6 22.2 %copy-start.5 = (bf16[128,16,32]{0,2,1:T(8,128)(2,1)S(1)}, bf16[128,16,32]{0,2,1:T(8,128)(2,1)}, u32[]{:S(2)}) copy-start(bf16[128,16,32]{0,2,1:T(8,128)(2,1)} %copy-done.4) | copy-start | bytes 393220 | tf_op jit(solution)/shard_map/while
  574.7 0.6 copy-start.4
  574.7 24.3 %all-gather.5.cloned.1.call-start = ((), (), s32[]{:S(2)}) async-start(), calls=%async_computation.3 | async-start | bytes 1179648 | tf_op jit(solution)/shard_map/while/body/eval_jaxpr/all_gather | solution.py:43
  575.3 62.7 %reduce-scatter.2.cloned.1.call-start = ((), (), s32[]{:S(2)}) async-start(), calls=%async_computation.4 | async-start | bytes 1310720 | tf_op jit(solution)/shard_map/while/body/eval_jaxpr/reduce_scatter | solution.py:27
  610.5 1.9 copy-start.2
  615.9 22.2 %copy-start.5 = (bf16[128,16,32]{0,2,1:T(8,128)(2,1)S(1)}, bf16[128,16,32]{0,2,1:T(8,128)(2,1)}, u32[]{:S(2)}) copy-start(bf16[128,16,32]{0,2,1:T(8,128)(2,1)} %copy-done.4) | copy-start | bytes 393220 | tf_op jit(solution)/shard_map/while
  647.9 1.9 copy-start.8
  647.9 133.3 %all-reduce.2.cloned.1.call-start = ((), (), s32[]{:S(2)}) async-start(), calls=%async_computation.1 | async-start | bytes 1048576 | tf_op jit(solution)/shard_map/psum | solution.py:68
  649.8 138.4 %copy-start.6 = (s32[8,128,128]{2,1,0:T(8,128)S(1)}, s32[8,128,128]{2,1,0:T(8,128)}, u32[]{:S(2)}) copy-start(s32[8,128,128]{2,1,0:T(8,128)} %param.16) | copy-start | bytes 1572868
  651.2 344.1 %all-gather.3.cloned.1.call-start = ((), (), s32[]{:S(2)}) async-start(), calls=%async_computation.2 | async-start | bytes 5242880 | tf_op jit(solution)/shard_map/all_gather | solution.py:98
  788.3 1.1 copy-start.7
  791.2 2.2 copy-start.3
  1073.1 33.7 %copy-start.1 = (s32[128,16,128]{2,1,0:T(8,128)S(1)}, s32[128,16,128]{2,1,0:T(8,128)}, u32[]{:S(2)}) copy-start(s32[128,16,128]{2,1,0:T(8,128)} %param.17) | copy-start | bytes 3145732
  (2 other events, 1.3 us)
Sparse Core Ops, SparseCore 0:
  58.6 26.0 all-gather.4
  96.5 27.2 reduce-scatter.1
  136.4 21.8 all-gather.4
  170.0 27.2 reduce-scatter.1
  209.6 21.8 all-gather.4
  243.3 27.2 reduce-scatter.1
  283.1 21.8 all-gather.4
  316.8 27.2 reduce-scatter.1
  356.7 21.8 all-gather.4
  390.4 27.2 reduce-scatter.1
  430.2 21.8 all-gather.4
  463.9 27.2 reduce-scatter.1
  503.8 21.8 all-gather.4
  537.5 27.2 reduce-scatter.1
  577.0 21.8 all-gather.4
  610.7 27.2 reduce-scatter.1
Sparse Core Ops, SparseCore 1:
  654.2 126.9 all-reduce.1
  915.6 79.7 all-gather.2
where the time goes:
time: 1120 us; the launch traced here: 1110 us
  waiting for transfers between devices  570 us (51%)
  local copies, waits for them, and re-layouts  279 us (25%)
  matrix products  122 us (11%)
  other arithmetic  87.2 us (8%)
  blocking collectives  39.1 us (3%)
  between operations  16 us (1%)
    all_gather x8, waiting for transfers between devices, advance(): lax.all_gather(pulse_output, 'row', axis=1, tiled=True).reshape(batch, -1)  194 us
    reduce_scatter x8, waiting for transfers between devices, combine_currents(): lax.psum_scatter(partial_value, 'col', scatter_dimension=2, tiled=True)  166 us
    dynamic_update_slice x40, local copies, waits for them, and re-layouts, body(): lax.scan(advance, (start_spikes, zeros, zeros, trace_zero), external)  140 us
    psum x1, waiting for transfers between devices, body(): lax.psum(jnp.dot(spikes.reshape(rows_all, -1), readout_loc, preferred_ele...  129 us
    dot_general x8, matrix products, advance(): jnp.dot(arrivals, weights, preferred_element_type=jnp.float32)  92.8 us
    all_gather x1, waiting for transfers between devices, body(): lax.all_gather(factors.reshape(rows_all, rows_loc, state_cols), 'col', ax...  79.8 us
    unnamed x24, local copies, waits for them, and re-layouts  77.5 us
    dynamic_slice x32, local copies, waits for them, and re-layouts, body(): lax.scan(advance, (start_spikes, zeros, zeros, trace_zero), external)  44.8 us
  transfers between devices with their start and end apart: 18, of which 18 were waited for; matrix products, arithmetic and copies ran while one was open for 5% of the time, Pallas kernels for 0%

commit v1 on v0

--- a/solution.py
+++ b/solution.py
@@ -65,10 +65,11 @@
         advance, (start_spikes, zeros, zeros, trace_zero), external
     )
     readout_loc = own_part(w_out, 1).reshape(rows_loc * own_cols, -1)
-    projected = lax.psum(
-        jnp.dot(spikes.reshape(rows_all, -1), readout_loc, preferred_element_type=jnp.float32),
-        ("row", "col"),
+    projected = jnp.dot(
+        spikes.reshape(rows_all, -1), readout_loc, preferred_element_type=jnp.float32
     )
+    for name in ("col", "row"):
+        projected = lax.psum(projected, name)
     outputs_n = readout_loc.shape[1]
     projected = projected.reshape(steps_count, batch, outputs_n)
 

time: 1120 us -> 1080 us (0.964)
  waiting for transfers between devices: 570 us -> 534 us
    psum x1 -> x2, waiting for transfers between devices: 129 us -> 93.3 us  [body(): projected = lax.psum(projected, name)]
  transfers between devices with their start and end apart: 18 -> 19, of which waited for: 18 -> 19; matrix products, arithmetic and copies ran while one was open for 5% -> 5% of each run, Pallas kernels for 0% -> 0%
where the time goes in v1:
time: 1080 us
  waiting for transfers between devices  534 us (49%)
  local copies, waits for them, and re-layouts  279 us (26%)
  matrix products  122 us (11%)
  other arithmetic  87.2 us (8%)
  blocking collectives  39.1 us (4%)
  between operations  16.3 us (2%)
    all_gather x8, waiting for transfers between devices, advance(): lax.all_gather(pulse_output, 'row', axis=1, tiled=True).reshape(batch, -1)  194 us
    reduce_scatter x8, waiting for transfers between devices, combine_currents(): lax.psum_scatter(partial_value, 'col', scatter_dimension=2, tiled=True)  166 us
    dynamic_update_slice x40, local copies, waits for them, and re-layouts, body(): lax.scan(advance, (start_spikes, zeros, zeros, trace_zero), external)  140 us
    psum x2, waiting for transfers between devices, body(): projected = lax.psum(projected, name)  93.3 us
    dot_general x8, matrix products, advance(): jnp.dot(arrivals, weights, preferred_element_type=jnp.float32)  92.8 us
    all_gather x1, waiting for transfers between devices, body(): lax.all_gather(factors.reshape(rows_all, rows_loc, state_cols), 'col', ax...  80.1 us
    unnamed x24, local copies, waits for them, and re-layouts  77.5 us
    dynamic_slice x32, local copies, waits for them, and re-layouts, body(): lax.scan(advance, (start_spikes, zeros, zeros, trace_zero), external)  44.8 us
  transfers between devices with their start and end apart: 19, of which 19 were waited for; matrix products, arithmetic and copies ran while one was open for 5% of the time, Pallas kernels for 0%

profile of v1, /device:TPU:0, one launch (start us, length us, event | category | flops | bytes accessed | tf_op | source)
XLA Modules:
  0.0 1078.6 jit_solution(14633883422737261854)
XLA Ops:
  15.9 17.2 %copy.96 = bf16[512,8,16,128]{3,1,2,0:T(8,128)(2,1)} copy(bf16[512,8,16,128]{3,2,1,0:T(8,128)(2,1)} %bitcast.115) | data formatting | bytes 33554432
  33.1 21.2 %copy.58 = bf16[4096,2048]{0,1:T(8,128)(2,1)} copy(bf16[4096,2048]{1,0:T(8,128)(2,1)} %bitcast.112) | data formatting | bytes 33554432
  55.9 592.0 %while.55 = (s32[]{:T(128)}, bf16[128,16,32]{0,2,1:T(8,128)(2,1)S(1)}, f32[128,16,32]{0,2,1:T(8,128)S(1)}, f32[128,16,32]{0,2,1:T(8,128)S(1)}, f32[128,4096]{0,1...) while((s32[]{:T(128)}, ...), condition=%wide.region_2.3_spmd.clone, body=%wide.region_0.2_spmd.clone.sunk | while | flops 2151677952 | bytes 45881672 | solution.py:64
  56.7 28.0 %all-gather.5.cloned.1.call-done = bf16[128,128,32]{0,2,1:T(8,128)(2,1)} async-done(((bf16[128,16,32]{0,2,1:T(8,128)(2,1)}), bf16[128,128,32]{0,2,1:T(8,128)(2,1)}) %all-gather.5.cloned.1.call-update) | async-done | bytes 1048592 | tf_op jit(solution)/shard_map/while/body/eval_jaxpr/all_gather | solution.py:43
  84.7 11.6 %fusion.29 = f32[128,16,128]{0,2,1:T(8,128)} fusion(bf16[128,4096,1]{0,1,2:T(8,128)(2,1)} %bitcast.111, bf16[16,128,4096]{2,1,0:T(8,128)(2,1)} %bitcast.109), kind=kOutput, calls=%fused_computation.43.clone.1 | convolution fusion | flops 2147483648 | bytes 18874368 | tf_op jit(solution)/shard_map/while/body/eval_jaxpr/dot_general | solution.py:45
  101.7 22.1 %reduce-scatter.2.cloned.1.call-done = f32[128,16,32]{0,2,1:T(8,128)} async-done(((f32[128,16,128]{0,2,1:T(8,128)}), f32[128,16,32]{0,2,1:T(8,128)}) %reduce-scatter.2.cloned.1.call-update) | async-done | bytes 262160 | tf_op jit(solution)/shard_map/while/body/eval_jaxpr/reduce_scatter | solution.py:27
  126.0 7.7 dynamic_update_slice.49
  134.5 23.8 %all-gather.5.cloned.1.call-done = bf16[128,128,32]{0,2,1:T(8,128)(2,1)} async-done(((bf16[128,16,32]{0,2,1:T(8,128)(2,1)}), bf16[128,128,32]{0,2,1:T(8,128)(2,1)}) %all-gather.5.cloned.1.call-update) | async-done | bytes 1048592 | tf_op jit(solution)/shard_map/while/body/eval_jaxpr/all_gather | solution.py:43
  158.3 11.6 %fusion.29 = f32[128,16,128]{0,2,1:T(8,128)} fusion(bf16[128,4096,1]{0,1,2:T(8,128)(2,1)} %bitcast.111, bf16[16,128,4096]{2,1,0:T(8,128)(2,1)} %bitcast.109), kind=kOutput, calls=%fused_computation.43.clone.1 | convolution fusion | flops 2147483648 | bytes 18874368 | tf_op jit(solution)/shard_map/while/body/eval_jaxpr/dot_general | solution.py:45
  176.8 20.5 %reduce-scatter.2.cloned.1.call-done = f32[128,16,32]{0,2,1:T(8,128)} async-done(((f32[128,16,128]{0,2,1:T(8,128)}), f32[128,16,32]{0,2,1:T(8,128)}) %reduce-scatter.2.cloned.1.call-update) | async-done | bytes 262160 | tf_op jit(solution)/shard_map/while/body/eval_jaxpr/reduce_scatter | solution.py:27
  199.5 7.7 dynamic_update_slice.49
  207.9 23.6 %all-gather.5.cloned.1.call-done = bf16[128,128,32]{0,2,1:T(8,128)(2,1)} async-done(((bf16[128,16,32]{0,2,1:T(8,128)(2,1)}), bf16[128,128,32]{0,2,1:T(8,128)(2,1)}) %all-gather.5.cloned.1.call-update) | async-done | bytes 1048592 | tf_op jit(solution)/shard_map/while/body/eval_jaxpr/all_gather | solution.py:43
  231.5 11.6 %fusion.29 = f32[128,16,128]{0,2,1:T(8,128)} fusion(bf16[128,4096,1]{0,1,2:T(8,128)(2,1)} %bitcast.111, bf16[16,128,4096]{2,1,0:T(8,128)(2,1)} %bitcast.109), kind=kOutput, calls=%fused_computation.43.clone.1 | convolution fusion | flops 2147483648 | bytes 18874368 | tf_op jit(solution)/shard_map/while/body/eval_jaxpr/dot_general | solution.py:45
  250.1 20.5 %reduce-scatter.2.cloned.1.call-done = f32[128,16,32]{0,2,1:T(8,128)} async-done(((f32[128,16,128]{0,2,1:T(8,128)}), f32[128,16,32]{0,2,1:T(8,128)}) %reduce-scatter.2.cloned.1.call-update) | async-done | bytes 262160 | tf_op jit(solution)/shard_map/while/body/eval_jaxpr/reduce_scatter | solution.py:27
  272.7 7.7 dynamic_update_slice.49
  281.2 23.8 %all-gather.5.cloned.1.call-done = bf16[128,128,32]{0,2,1:T(8,128)(2,1)} async-done(((bf16[128,16,32]{0,2,1:T(8,128)(2,1)}), bf16[128,128,32]{0,2,1:T(8,128)(2,1)}) %all-gather.5.cloned.1.call-update) | async-done | bytes 1048592 | tf_op jit(solution)/shard_map/while/body/eval_jaxpr/all_gather | solution.py:43
  305.1 11.6 %fusion.29 = f32[128,16,128]{0,2,1:T(8,128)} fusion(bf16[128,4096,1]{0,1,2:T(8,128)(2,1)} %bitcast.111, bf16[16,128,4096]{2,1,0:T(8,128)(2,1)} %bitcast.109), kind=kOutput, calls=%fused_computation.43.clone.1 | convolution fusion | flops 2147483648 | bytes 18874368 | tf_op jit(solution)/shard_map/while/body/eval_jaxpr/dot_general | solution.py:45
  323.6 20.5 %reduce-scatter.2.cloned.1.call-done = f32[128,16,32]{0,2,1:T(8,128)} async-done(((f32[128,16,128]{0,2,1:T(8,128)}), f32[128,16,32]{0,2,1:T(8,128)}) %reduce-scatter.2.cloned.1.call-update) | async-done | bytes 262160 | tf_op jit(solution)/shard_map/while/body/eval_jaxpr/reduce_scatter | solution.py:27
  346.3 7.7 dynamic_update_slice.49
  354.8 23.8 %all-gather.5.cloned.1.call-done = bf16[128,128,32]{0,2,1:T(8,128)(2,1)} async-done(((bf16[128,16,32]{0,2,1:T(8,128)(2,1)}), bf16[128,128,32]{0,2,1:T(8,128)(2,1)}) %all-gather.5.cloned.1.call-update) | async-done | bytes 1048592 | tf_op jit(solution)/shard_map/while/body/eval_jaxpr/all_gather | solution.py:43
  378.6 11.6 %fusion.29 = f32[128,16,128]{0,2,1:T(8,128)} fusion(bf16[128,4096,1]{0,1,2:T(8,128)(2,1)} %bitcast.111, bf16[16,128,4096]{2,1,0:T(8,128)(2,1)} %bitcast.109), kind=kOutput, calls=%fused_computation.43.clone.1 | convolution fusion | flops 2147483648 | bytes 18874368 | tf_op jit(solution)/shard_map/while/body/eval_jaxpr/dot_general | solution.py:45
  397.2 20.5 %reduce-scatter.2.cloned.1.call-done = f32[128,16,32]{0,2,1:T(8,128)} async-done(((f32[128,16,128]{0,2,1:T(8,128)}), f32[128,16,32]{0,2,1:T(8,128)}) %reduce-scatter.2.cloned.1.call-update) | async-done | bytes 262160 | tf_op jit(solution)/shard_map/while/body/eval_jaxpr/reduce_scatter | solution.py:27
  419.9 7.7 dynamic_update_slice.49
  428.3 23.8 %all-gather.5.cloned.1.call-done = bf16[128,128,32]{0,2,1:T(8,128)(2,1)} async-done(((bf16[128,16,32]{0,2,1:T(8,128)(2,1)}), bf16[128,128,32]{0,2,1:T(8,128)(2,1)}) %all-gather.5.cloned.1.call-update) | async-done | bytes 1048592 | tf_op jit(solution)/shard_map/while/body/eval_jaxpr/all_gather | solution.py:43
  452.2 11.6 %fusion.29 = f32[128,16,128]{0,2,1:T(8,128)} fusion(bf16[128,4096,1]{0,1,2:T(8,128)(2,1)} %bitcast.111, bf16[16,128,4096]{2,1,0:T(8,128)(2,1)} %bitcast.109), kind=kOutput, calls=%fused_computation.43.clone.1 | convolution fusion | flops 2147483648 | bytes 18874368 | tf_op jit(solution)/shard_map/while/body/eval_jaxpr/dot_general | solution.py:45
  470.7 20.5 %reduce-scatter.2.cloned.1.call-done = f32[128,16,32]{0,2,1:T(8,128)} async-done(((f32[128,16,128]{0,2,1:T(8,128)}), f32[128,16,32]{0,2,1:T(8,128)}) %reduce-scatter.2.cloned.1.call-update) | async-done | bytes 262160 | tf_op jit(solution)/shard_map/while/body/eval_jaxpr/reduce_scatter | solution.py:27
  493.4 7.7 dynamic_update_slice.49
  501.9 23.8 %all-gather.5.cloned.1.call-done = bf16[128,128,32]{0,2,1:T(8,128)(2,1)} async-done(((bf16[128,16,32]{0,2,1:T(8,128)(2,1)}), bf16[128,128,32]{0,2,1:T(8,128)(2,1)}) %all-gather.5.cloned.1.call-update) | async-done | bytes 1048592 | tf_op jit(solution)/shard_map/while/body/eval_jaxpr/all_gather | solution.py:43
  525.7 11.6 %fusion.29 = f32[128,16,128]{0,2,1:T(8,128)} fusion(bf16[128,4096,1]{0,1,2:T(8,128)(2,1)} %bitcast.111, bf16[16,128,4096]{2,1,0:T(8,128)(2,1)} %bitcast.109), kind=kOutput, calls=%fused_computation.43.clone.1 | convolution fusion | flops 2147483648 | bytes 18874368 | tf_op jit(solution)/shard_map/while/body/eval_jaxpr/dot_general | solution.py:45
  544.2 20.6 %reduce-scatter.2.cloned.1.call-done = f32[128,16,32]{0,2,1:T(8,128)} async-done(((f32[128,16,128]{0,2,1:T(8,128)}), f32[128,16,32]{0,2,1:T(8,128)}) %reduce-scatter.2.cloned.1.call-update) | async-done | bytes 262160 | tf_op jit(solution)/shard_map/while/body/eval_jaxpr/reduce_scatter | solution.py:27
  566.9 7.7 dynamic_update_slice.49
  575.4 23.6 %all-gather.5.cloned.1.call-done = bf16[128,128,32]{0,2,1:T(8,128)(2,1)} async-done(((bf16[128,16,32]{0,2,1:T(8,128)(2,1)}), bf16[128,128,32]{0,2,1:T(8,128)(2,1)}) %all-gather.5.cloned.1.call-update) | async-done | bytes 1048592 | tf_op jit(solution)/shard_map/while/body/eval_jaxpr/all_gather | solution.py:43
  598.9 11.6 %fusion.29 = f32[128,16,128]{0,2,1:T(8,128)} fusion(bf16[128,4096,1]{0,1,2:T(8,128)(2,1)} %bitcast.111, bf16[16,128,4096]{2,1,0:T(8,128)(2,1)} %bitcast.109), kind=kOutput, calls=%fused_computation.43.clone.1 | convolution fusion | flops 2147483648 | bytes 18874368 | tf_op jit(solution)/shard_map/while/body/eval_jaxpr/dot_general | solution.py:45
  617.5 20.5 %reduce-scatter.2.cloned.1.call-done = f32[128,16,32]{0,2,1:T(8,128)} async-done(((f32[128,16,128]{0,2,1:T(8,128)}), f32[128,16,32]{0,2,1:T(8,128)}) %reduce-scatter.2.cloned.1.call-update) | async-done | bytes 262160 | tf_op jit(solution)/shard_map/while/body/eval_jaxpr/reduce_scatter | solution.py:27
  640.2 7.7 dynamic_update_slice.49
  651.4 37.1 %all-reduce.3.cloned.1.call-done = f32[1024,128]{1,0:T(8,128)} async-done(((f32[1024,128]{1,0:T(8,128)}), f32[1024,128]{1,0:T(8,128)}) %all-reduce.3.cloned.1.call-update) | async-done | bytes 524304 | tf_op jit(solution)/shard_map/psum | solution.py:72
  689.1 56.2 %all-reduce.5.cloned.1.call-done = f32[8,128,128]{2,1,0:T(8,128)} async-done(((f32[8,128,128]{2,1,0:T(8,128)}), f32[8,128,128]{2,1,0:T(8,128)}) %all-reduce.5.cloned.1.call-update) | async-done | bytes 524304 | tf_op jit(solution)/shard_map/psum | solution.py:72
  762.3 112.8 %while.57 = (s32[]{:T(128)}, f32[128,16,32]{2,1,0:T(8,128)}, f32[8,128,16,32]{1,0,3,2:T(8,128)}, f32[8,128,16,32]{1,0,3,2:T(8,128)}, f32[8,128,16,32]{1,0,3,2:T(8,128)}, /*index=5*/s32[]{:T(128)}, s32[]{:T(128)}, s32[]{:T(128)}) while((s32[]{:T(128)}, f32[128,16,32]{2,1,0:T(8,128)}, f32[8,128,16,32]{1,0,3,2:T(8,128)}, ...), condition=%wide.region_8.9_spmd.clone, body=%wide.region_7.8_spmd.clone.sunk | while | flops 196612 | bytes 4456571 | solution.py:96
  767.6 7.7 dynamic_update_slice.51
  796.2 7.7 dynamic_update_slice.51
  810.4 7.7 dynamic_update_slice.51
  824.7 7.7 dynamic_update_slice.51
  838.9 7.7 dynamic_update_slice.51
  879.6 80.1 %all-gather.3.cloned.1.call-done = bf16[1024,16,128]{0,2,1:T(8,128)(2,1)} async-done(((bf16[1024,16,32]{0,2,1:T(8,128)(2,1)}), bf16[1024,16,128]{0,2,1:T(8,128)(2,1)}) %all-gather.3.cloned.1.call-update) | async-done | bytes 4194320 | tf_op jit(solution)/shard_map/all_gather | solution.py:99
  959.7 26.1 %multiply_reduce_fusion = (f32[]{:T(128)}, f32[4096,16,128]{2,0,1:T(8,128)}) fusion(bf16[1024,4096,1]{1,0,2:T(8,128)(2,1)} %bitcast.128, bf16[1024,16,128]{0,2,1:T(8,128)(2,1)} %all-gather.3.cloned.1.call-done), kind=kOutput, calls=%fused_computation.22 | convolution fusion | flops 17196646400 | bytes 46137348 | tf_op jit(solution)/shard_map/dot_general | solution.py:102
  985.9 39.1 %psum.23 = f32[]{:T(128)} all-reduce(f32[]{:T(128)} %get-tuple-element.484), channel_id=1, replica_groups=mesh['row'=8,'col'=4] {'row','col'}, use_global_device_ids=true, to_apply=%region_10.11 | all-reduce | flops 1 | bytes 8 | tf_op jit(solution)/shard_map/psum | solution.py:109
  1025.6 11.9 %broadcast_multiply_fusion = f32[4096,16,128]{2,0,1:T(8,128)S(1)} fusion(f32[4096,16,128]{2,0,1:T(8,128)} %get-tuple-element.485, f32[]{:T(128)S(6)} %min.3), kind=kLoop, calls=%fused_computation.24 | loop fusion | flops 8388608 | bytes 67108864 | tf_op jit(solution)/shard_map/mul | solution.py:111
  1037.5 33.7 %copy.69 = f32[128,32,16,128]{3,2,1,0:T(8,128)} copy(f32[128,32,16,128]{3,1,0,2:T(8,128)S(1)} %bitcast.110) | data formatting | bytes 67108864
  (233 shorter events, 192.8 us)
Async XLA Ops:
  8.0 2.8 copy-start
  33.1 21.2 %copy-start.9 = (f32[16,128]{1,0:T(8,128)S(1)}, f32[16,128]{1,0:T(8,128)}, u32[]{:S(2)}) copy-start(f32[16,128]{1,0:T(8,128)} %param.23) | copy-start | bytes 24580
  33.1 21.2 %copy-start.10 = (f32[16,128]{1,0:T(8,128)S(1)}, f32[16,128]{1,0:T(8,128)}, u32[]{:S(2)}) copy-start(f32[16,128]{1,0:T(8,128)} %param.22) | copy-start | bytes 24580
  55.9 28.8 %all-gather.5.cloned.1.call-start = ((), (), s32[]{:S(2)}) async-start(), calls=%async_computation.4 | async-start | bytes 1179648 | tf_op jit(solution)/shard_map/while/body/eval_jaxpr/all_gather | solution.py:43
  56.6 67.2 %reduce-scatter.2.cloned.1.call-start = ((), (), s32[]{:S(2)}) async-start(), calls=%async_computation.5 | async-start | bytes 1310720 | tf_op jit(solution)/shard_map/while/body/eval_jaxpr/reduce_scatter | solution.py:27
  96.3 1.9 copy-start.2
  100.1 23.7 %copy-start.5 = (bf16[128,16,32]{0,2,1:T(8,128)(2,1)S(1)}, bf16[128,16,32]{0,2,1:T(8,128)(2,1)}, u32[]{:S(2)}) copy-start(bf16[128,16,32]{0,2,1:T(8,128)(2,1)} %copy-done.4) | copy-start | bytes 393220 | tf_op jit(solution)/shard_map/while
  133.7 0.6 copy-start.4
  133.7 24.6 %all-gather.5.cloned.1.call-start = ((), (), s32[]{:S(2)}) async-start(), calls=%async_computation.4 | async-start | bytes 1179648 | tf_op jit(solution)/shard_map/while/body/eval_jaxpr/all_gather | solution.py:43
  134.4 62.9 %reduce-scatter.2.cloned.1.call-start = ((), (), s32[]{:S(2)}) async-start(), calls=%async_computation.5 | async-start | bytes 1310720 | tf_op jit(solution)/shard_map/while/body/eval_jaxpr/reduce_scatter | solution.py:27
  169.9 1.9 copy-start.2
  175.2 22.2 %copy-start.5 = (bf16[128,16,32]{0,2,1:T(8,128)(2,1)S(1)}, bf16[128,16,32]{0,2,1:T(8,128)(2,1)}, u32[]{:S(2)}) copy-start(bf16[128,16,32]{0,2,1:T(8,128)(2,1)} %copy-done.4) | copy-start | bytes 393220 | tf_op jit(solution)/shard_map/while
  207.2 0.6 copy-start.4
  207.2 24.3 %all-gather.5.cloned.1.call-start = ((), (), s32[]{:S(2)}) async-start(), calls=%async_computation.4 | async-start | bytes 1179648 | tf_op jit(solution)/shard_map/while/body/eval_jaxpr/all_gather | solution.py:43
  207.9 62.7 %reduce-scatter.2.cloned.1.call-start = ((), (), s32[]{:S(2)}) async-start(), calls=%async_computation.5 | async-start | bytes 1310720 | tf_op jit(solution)/shard_map/while/body/eval_jaxpr/reduce_scatter | solution.py:27
  243.1 1.9 copy-start.2
  248.4 22.2 %copy-start.5 = (bf16[128,16,32]{0,2,1:T(8,128)(2,1)S(1)}, bf16[128,16,32]{0,2,1:T(8,128)(2,1)}, u32[]{:S(2)}) copy-start(bf16[128,16,32]{0,2,1:T(8,128)(2,1)} %copy-done.4) | copy-start | bytes 393220 | tf_op jit(solution)/shard_map/while
  280.5 0.6 copy-start.4
  280.5 24.6 %all-gather.5.cloned.1.call-start = ((), (), s32[]{:S(2)}) async-start(), calls=%async_computation.4 | async-start | bytes 1179648 | tf_op jit(solution)/shard_map/while/body/eval_jaxpr/all_gather | solution.py:43
  281.2 62.9 %reduce-scatter.2.cloned.1.call-start = ((), (), s32[]{:S(2)}) async-start(), calls=%async_computation.5 | async-start | bytes 1310720 | tf_op jit(solution)/shard_map/while/body/eval_jaxpr/reduce_scatter | solution.py:27
  316.7 1.9 copy-start.2
  322.0 22.2 %copy-start.5 = (bf16[128,16,32]{0,2,1:T(8,128)(2,1)S(1)}, bf16[128,16,32]{0,2,1:T(8,128)(2,1)}, u32[]{:S(2)}) copy-start(bf16[128,16,32]{0,2,1:T(8,128)(2,1)} %copy-done.4) | copy-start | bytes 393220 | tf_op jit(solution)/shard_map/while
  354.0 0.6 copy-start.4
  354.0 24.6 %all-gather.5.cloned.1.call-start = ((), (), s32[]{:S(2)}) async-start(), calls=%async_computation.4 | async-start | bytes 1179648 | tf_op jit(solution)/shard_map/while/body/eval_jaxpr/all_gather | solution.py:43
  354.7 62.9 %reduce-scatter.2.cloned.1.call-start = ((), (), s32[]{:S(2)}) async-start(), calls=%async_computation.5 | async-start | bytes 1310720 | tf_op jit(solution)/shard_map/while/body/eval_jaxpr/reduce_scatter | solution.py:27
  390.2 1.9 copy-start.2
  395.5 22.2 %copy-start.5 = (bf16[128,16,32]{0,2,1:T(8,128)(2,1)S(1)}, bf16[128,16,32]{0,2,1:T(8,128)(2,1)}, u32[]{:S(2)}) copy-start(bf16[128,16,32]{0,2,1:T(8,128)(2,1)} %copy-done.4) | copy-start | bytes 393220 | tf_op jit(solution)/shard_map/while
  427.6 24.6 %all-gather.5.cloned.1.call-start = ((), (), s32[]{:S(2)}) async-start(), calls=%async_computation.4 | async-start | bytes 1179648 | tf_op jit(solution)/shard_map/while/body/eval_jaxpr/all_gather | solution.py:43
  428.3 62.9 %reduce-scatter.2.cloned.1.call-start = ((), (), s32[]{:S(2)}) async-start(), calls=%async_computation.5 | async-start | bytes 1310720 | tf_op jit(solution)/shard_map/while/body/eval_jaxpr/reduce_scatter | solution.py:27
  463.8 1.9 copy-start.2
  469.1 22.2 %copy-start.5 = (bf16[128,16,32]{0,2,1:T(8,128)(2,1)S(1)}, bf16[128,16,32]{0,2,1:T(8,128)(2,1)}, u32[]{:S(2)}) copy-start(bf16[128,16,32]{0,2,1:T(8,128)(2,1)} %copy-done.4) | copy-start | bytes 393220 | tf_op jit(solution)/shard_map/while
  501.1 0.6 copy-start.4
  501.1 24.6 %all-gather.5.cloned.1.call-start = ((), (), s32[]{:S(2)}) async-start(), calls=%async_computation.4 | async-start | bytes 1179648 | tf_op jit(solution)/shard_map/while/body/eval_jaxpr/all_gather | solution.py:43
  501.8 62.9 %reduce-scatter.2.cloned.1.call-start = ((), (), s32[]{:S(2)}) async-start(), calls=%async_computation.5 | async-start | bytes 1310720 | tf_op jit(solution)/shard_map/while/body/eval_jaxpr/reduce_scatter | solution.py:27
  537.3 1.9 copy-start.2
  542.6 22.2 %copy-start.5 = (bf16[128,16,32]{0,2,1:T(8,128)(2,1)S(1)}, bf16[128,16,32]{0,2,1:T(8,128)(2,1)}, u32[]{:S(2)}) copy-start(bf16[128,16,32]{0,2,1:T(8,128)(2,1)} %copy-done.4) | copy-start | bytes 393220 | tf_op jit(solution)/shard_map/while
  574.7 24.3 %all-gather.5.cloned.1.call-start = ((), (), s32[]{:S(2)}) async-start(), calls=%async_computation.4 | async-start | bytes 1179648 | tf_op jit(solution)/shard_map/while/body/eval_jaxpr/all_gather | solution.py:43
  575.3 62.7 %reduce-scatter.2.cloned.1.call-start = ((), (), s32[]{:S(2)}) async-start(), calls=%async_computation.5 | async-start | bytes 1310720 | tf_op jit(solution)/shard_map/while/body/eval_jaxpr/reduce_scatter | solution.py:27
  610.5 1.9 copy-start.2
  615.9 22.2 %copy-start.5 = (bf16[128,16,32]{0,2,1:T(8,128)(2,1)S(1)}, bf16[128,16,32]{0,2,1:T(8,128)(2,1)}, u32[]{:S(2)}) copy-start(bf16[128,16,32]{0,2,1:T(8,128)(2,1)} %copy-done.4) | copy-start | bytes 393220 | tf_op jit(solution)/shard_map/while
  647.9 1.9 copy-start.8
  647.9 40.6 %all-reduce.3.cloned.1.call-start = ((), (), s32[]{:S(2)}) async-start(), calls=%async_computation.1 | async-start | bytes 1048576 | tf_op jit(solution)/shard_map/psum | solution.py:72
  649.8 102.6 %copy-start.6 = (s32[8,128,128]{2,1,0:T(8,128)S(1)}, s32[8,128,128]{2,1,0:T(8,128)}, u32[]{:S(2)}) copy-start(s32[8,128,128]{2,1,0:T(8,128)} %param.16) | copy-start | bytes 1572868
  651.2 94.1 %all-reduce.5.cloned.1.call-start = ((), (), s32[]{:S(2)}) async-start(), calls=%async_computation.2 | async-start | bytes 1048576 | tf_op jit(solution)/shard_map/psum | solution.py:72
  688.5 271.2 %all-gather.3.cloned.1.call-start = ((), (), s32[]{:S(2)}) async-start(), calls=%async_computation.3 | async-start | bytes 5242880 | tf_op jit(solution)/shard_map/all_gather | solution.py:99
  752.4 1.1 copy-start.7
  755.4 2.2 copy-start.3
  1037.5 33.7 %copy-start.1 = (s32[128,16,128]{2,1,0:T(8,128)S(1)}, s32[128,16,128]{2,1,0:T(8,128)}, u32[]{:S(2)}) copy-start(s32[128,16,128]{2,1,0:T(8,128)} %param.17) | copy-start | bytes 3145732
  (3 other events, 1.9 us)
Sparse Core Ops, SparseCore 0:
  58.6 26.0 all-gather.4
  96.5 27.2 reduce-scatter.1
  136.4 21.8 all-gather.4
  170.0 27.2 reduce-scatter.1
  209.6 21.8 all-gather.4
  243.3 27.2 reduce-scatter.1
  283.1 21.8 all-gather.4
  316.8 27.2 reduce-scatter.1
  356.7 21.8 all-gather.4
  390.4 27.2 reduce-scatter.1
  430.2 21.8 all-gather.4
  463.9 27.2 reduce-scatter.1
  503.8 21.8 all-gather.4
  537.5 27.2 reduce-scatter.1
  577.0 21.8 all-gather.4
  610.7 27.2 reduce-scatter.1
Sparse Core Ops, SparseCore 1:
  651.3 37.2 all-reduce.2
  691.5 53.8 all-reduce.4
  879.7 80.0 all-gather.2
